TPU v7x, 32 devices: a whole 2x2x4 slice. The times are simulated.
32 devices in a mesh: dp: 4 (over y, core), expert: 4 (over z), tensor: 2 (over x).
Axes of the slice: x: 2, y: 2, z: 4, core: 2. Of those that a mesh axis runs over, the one named last changes fastest.
Arguments:
- tokens: bfloat16 [256, 3072], P(('dp', 'expert')), may hold values from -45 to 45
- cotangent: bfloat16 [256, 3072], P(('dp', 'expert')), may hold values from -6 to 6
- gain: float32 [3072], replicated, may hold values from 0.5 to 1.5
- w_router: bfloat16 [3072, 4], replicated, may hold values from -0.109375 to 0.109375
- w_gate: bfloat16 [4, 3072, 9216], P('expert', None, 'tensor'), may hold values from -0.109375 to 0.109375
- w_up: bfloat16 [4, 3072, 9216], P('expert', None, 'tensor'), may hold values from -0.109375 to 0.109375
- w_down: bfloat16 [4, 9216, 3072], P('expert', 'tensor'), may hold values from -0.0625 to 0.0625
- expert_ids: int32 [256, 2], P(('dp', 'expert')), may hold values from 0 to 3, as said below
- slots: int32 [256, 2], P(('dp', 'expert')), may hold values from 0 to 7, as said below
Outputs:
- mixed: bfloat16 [256, 3072], P(('dp', 'expert'))
- grad_tokens: bfloat16 [256, 3072], P(('dp', 'expert'))
- grad_router: float32 [3072, 4], replicated
- grad_gain: float32 [3072], replicated
Inputs may be any that keep to these rules, and one draw needn't show every extreme that they name: `expert_ids`: within each aligned block of 16 rows (one group), every expert is named exactly 8 times, and a row's two ids differ. Within each aligned block of 16 rows, the choices naming one expert hold its slots 0 to 7, each once.
All inputs are finite; a program needn't handle non-finite values.
Results may differ from a plain program's by a relative error of at most 0.0095.
Values may be sent and summed in bfloat16 or wider, within the bound.
No kernel may reach another device: no remote copies, remote signals or barrier semaphores. Data moves between devices by JAX's collectives and lax.ppermute only.
A program may use at most 128 MiB of HBM per device.

v0:
```python
import jax
import jax.numpy as jnp
from jax import lax
from jax.sharding import PartitionSpec as P

epsilon = 1e-05


def pack_rows(select, values):
    return jnp.einsum("tcr,tcd->rd", select, values, preferred_element_type=jnp.float32).astype(
        jnp.bfloat16
    )


def repeat_blocks(packed, experts, copies):
    feature_width = packed.shape[1]
    blocks = packed.reshape(experts, 1, -1, feature_width)
    blocks = jnp.broadcast_to(blocks, (experts, copies, blocks.shape[2], feature_width))
    return blocks.reshape(experts * copies, -1, feature_width)


def to_experts(packed, experts, copies):
    arrived = lax.all_to_all(
        repeat_blocks(packed, experts, copies), "expert", split_axis=0, concat_axis=0, tiled=True
    )
    return arrived.reshape(-1, packed.shape[1])


def from_experts(partial_value, row_index, experts, copies):
    partial_value = lax.psum_scatter(
        partial_value.astype(jnp.bfloat16), "tensor", scatter_dimension=1, tiled=True
    ).astype(jnp.float32)
    feature_width = partial_value.shape[1]
    returned_rows = lax.all_to_all(
        partial_value.reshape(experts * copies, -1, feature_width),
        "expert",
        split_axis=0,
        concat_axis=0,
        tiled=True,
    )
    summed = jnp.sum(returned_rows.reshape(experts, copies, -1, feature_width), axis=1).reshape(
        -1, feature_width
    )
    picked = summed[row_index]
    picked = lax.all_gather(picked.astype(jnp.bfloat16), "tensor", axis=2, tiled=True).astype(
        picked.dtype
    )
    return picked


def shards(tokens, cotangent, gain, w_router, w_gate, w_up, w_down, expert_ids, slots):
    experts = w_router.shape[1]
    copies = lax.axis_size("expert") // experts
    token_count = tokens.shape[0]
    capacity = 2 * token_count // experts
    floats = tokens.astype(jnp.float32)
    inv_rms = lax.rsqrt(jnp.mean(floats * floats, axis=1, keepdims=True) + epsilon)
    normed = (floats * inv_rms * gain).astype(jnp.bfloat16)
    logits = jnp.dot(normed, w_router, preferred_element_type=jnp.float32)
    chosen_logits = jnp.take_along_axis(logits, expert_ids, axis=1)
    first_prob = jax.nn.sigmoid(chosen_logits[:, 0] - chosen_logits[:, 1])
    pair_probs = jnp.stack([first_prob, 1.0 - first_prob], axis=1)
    row_index = expert_ids * capacity + slots
    select = (
        row_index[:, :, None] == jnp.arange(experts * capacity, dtype=jnp.int32)[None, None, :]
    ).astype(jnp.bfloat16)
    feature_width = tokens.shape[1]
    inputs = to_experts(
        pack_rows(select, jnp.broadcast_to(normed[:, None, :], (token_count, 2, feature_width))),
        experts,
        copies,
    )
    gate_matrix = w_gate[0]
    up_matrix = w_up[0]
    down_matrix = w_down[0]
    gate_pre = jnp.dot(inputs, gate_matrix, preferred_element_type=jnp.float32)
    up_pre = jnp.dot(inputs, up_matrix, preferred_element_type=jnp.float32)
    activated = (jax.nn.silu(gate_pre) * up_pre).astype(jnp.bfloat16)
    chosen = from_experts(
        jnp.dot(activated, down_matrix, preferred_element_type=jnp.float32),
        row_index,
        experts,
        copies,
    )
    mixed = (floats + jnp.sum(pair_probs[:, :, None] * chosen, axis=1)).astype(jnp.bfloat16)
    upstream = cotangent.astype(jnp.float32)
    sent_grads = (pair_probs[:, :, None] * upstream[:, None, :]).astype(jnp.bfloat16)
    grad_outputs = to_experts(pack_rows(select, sent_grads), experts, copies)
    grad_act = jnp.dot(grad_outputs, down_matrix.T, preferred_element_type=jnp.float32)
    sigmoid_gate = jax.nn.sigmoid(gate_pre)
    grad_gate = (grad_act * up_pre * sigmoid_gate * (1.0 + gate_pre * (1.0 - sigmoid_gate))).astype(
        jnp.bfloat16
    )
    grad_up = (grad_act * jax.nn.silu(gate_pre)).astype(jnp.bfloat16)
    grad_inputs = jnp.dot(grad_gate, gate_matrix.T, preferred_element_type=jnp.float32) + jnp.dot(
        grad_up, up_matrix.T, preferred_element_type=jnp.float32
    )
    grad_mixture = jnp.sum(from_experts(grad_inputs, row_index, experts, copies), axis=1)
    grad_probs = jnp.sum(upstream[:, None, :] * chosen, axis=2)
    grad_first = first_prob * (1.0 - first_prob) * (grad_probs[:, 0] - grad_probs[:, 1])
    columns = jnp.arange(experts, dtype=jnp.int32)[None, :]
    grad_logits = grad_first[:, None] * (
        (expert_ids[:, 0:1] == columns).astype(jnp.float32)
        - (expert_ids[:, 1:2] == columns).astype(jnp.float32)
    )
    grad_normed = grad_mixture + jnp.dot(
        grad_logits, w_router.astype(jnp.float32).T, precision=lax.Precision.HIGHEST
    )
    router_part = jnp.dot(
        normed.astype(jnp.float32).T, grad_logits, precision=lax.Precision.HIGHEST
    )
    gain_part = jnp.sum(grad_normed * floats * inv_rms, axis=0)
    grad_router, grad_gain = lax.psum((router_part, gain_part), ("dp", "expert"))
    grad_scaled = grad_normed * gain
    cubed = inv_rms * inv_rms * inv_rms
    grad_tokens = (
        upstream
        + inv_rms * grad_scaled
        - floats * cubed * jnp.mean(grad_scaled * floats, axis=1, keepdims=True)
    ).astype(jnp.bfloat16)
    return (mixed, grad_tokens, grad_router, grad_gain)


def solution(mesh):
    return jax.shard_map(
        shards,
        mesh=mesh,
        in_specs=(
            P(("dp", "expert"), None),
            P(("dp", "expert"), None),
            P(),
            P(),
            P("expert", None, "tensor"),
            P("expert", None, "tensor"),
            P("expert", "tensor", None),
            P(("dp", "expert"), None),
            P(("dp", "expert"), None),
        ),
        out_specs=(P(("dp", "expert"), None), P(("dp", "expert"), None), P(), P()),
        check_vma=False,
    )
```

profile of v0, /device:TPU:0, one launch (start us, length us, event | category | flops | bytes accessed | tf_op | source)
XLA Modules:
  0.0 204.1 jit_solution(13842822642820997463)
XLA Ops:
  7.2 0.0 copy-start
  7.2 1.0 fusion.29
  8.2 0.7 compare_select_fusion
  8.9 1.0 fusion.31
  9.9 1.0 fusion.24
  10.9 6.3 %all-to-all-start = ((bf16[4,8,3072]{2,1,0:T(8,128)(2,1)}), bf16[4,8,3072]{2,1,0:T(8,128)(2,1)S(1)}, u32[]{:S(2)}, u32[]{:S(2)}) async-start(bf16[4,8,3072]{2,1,0:T(8,128)(2,1)} %fusion.24), calls=%async_computation | async-start | bytes 393216 | tf_op jit(solution)/shard_map/all_to_all | solution.py:23
  17.3 0.7 bitcast_or_fusion
  17.9 0.1 copy.39
  18.0 0.1 reshape.101
  18.1 0.1 fusion.59
  18.3 0.8 gather_fusion.2
  19.0 0.1 reshape.104
  19.1 0.1 copy.40
  19.2 0.7 and_select_fusion
  19.9 0.9 convert_element_type.70
  20.8 1.0 fusion.23
  21.8 2.9 %all-to-all-done = bf16[4,8,3072]{2,1,0:T(8,128)(2,1)S(1)} async-done(((bf16[4,8,3072]{2,1,0:T(8,128)(2,1)}), bf16[4,8,3072]{2,1,0:T(8,128)(2,1)S(1)}, u32[]{:S(2)}, u32[]{:S(2)}) %all-to-all-start) | async-done | bytes 196640 | tf_op jit(solution)/shard_map/all_to_all | solution.py:23
  24.8 3.4 %all-to-all-start.2 = ((bf16[4,8,3072]{2,1,0:T(8,128)(2,1)}), bf16[4,8,3072]{2,1,0:T(8,128)(2,1)S(1)}, u32[]{:S(2)}, u32[]{:S(2)}) async-start(bf16[4,8,3072]{2,1,0:T(8,128)(2,1)} %fusion.23), calls=%async_computation.3 | async-start | bytes 393216 | tf_op jit(solution)/shard_map/all_to_all | solution.py:23
  28.1 0.0 reduce-scatter.3.cloned.1.call-start
  28.2 11.5 %fusion.10 = f32[32,4608]{1,0:T(8,128)S(1)} fusion(bf16[1,3072,4608]{2,1,0:T(8,128)(2,1)} %param.13, bf16[4,8,3072]{2,1,0:T(8,128)(2,1)S(1)} %all-to-all-done), kind=kOutput, calls=%fused_computation.13 | convolution fusion | flops 905969664 | bytes 29097984 | tf_op jit(solution)/shard_map/dot_general | solution.py:76
  39.7 11.5 %fusion.6 = f32[32,4608]{1,0:T(8,128)S(1)} fusion(bf16[1,3072,4608]{2,1,0:T(8,128)(2,1)} %param.14, bf16[4,8,3072]{2,1,0:T(8,128)(2,1)S(1)} %all-to-all-done), kind=kOutput, calls=%fused_computation.9 | convolution fusion | flops 905969664 | bytes 29097984 | tf_op jit(solution)/shard_map/dot_general | solution.py:77
  51.2 12.3 %fusion.20 = bf16[32,3072]{1,0:T(8,128)(2,1)} fusion(bf16[1,4608,3072]{2,1,0:T(8,128)(2,1)} %param.15, f32[32,4608]{1,0:T(8,128)S(1)} %fusion.6, f32[32,4608]{1,0:T(8,128)S(1)} %fusion.10), kind=kOutput, calls=%fused_computation.21 | convolution fusion | flops 906952704 | bytes 29687808 | tf_op jit(solution)/shard_map/dot_general | solution.py:80
  63.6 0.0 reduce-scatter.3.cloned.1.call-update
  63.6 0.2 reduce-scatter.5.cloned.1.call-start
  63.8 0.0 all-to-all-done.2
  63.8 13.6 %fusion = f32[32,4608]{1,0:T(8,128)S(1)} fusion(bf16[1,4608,3072]{2,1,0:T(8,128)(2,1)} %param.15, bf16[4,8,3072]{2,1,0:T(8,128)(2,1)S(1)} %all-to-all-done.2), kind=kOutput, calls=%fused_computation.3 | convolution fusion | flops 905969664 | bytes 29097984 | tf_op jit(solution)/shard_map/dot_general | solution.py:89
  77.4 13.5 %fusion.4 = f32[32,3072]{1,0:T(8,128)S(1)} fusion(bf16[1,3072,4608]{2,1,0:T(8,128)(2,1)} %param.14, f32[32,4608]{1,0:T(8,128)S(1)} %fusion, f32[32,4608]{1,0:T(8,128)S(1)} %fusion.10), kind=kOutput, calls=%fused_computation.7 | convolution fusion | flops 906854400 | bytes 29884416 | tf_op jit(solution)/shard_map/dot_general | solution.py:95
  90.9 0.0 copy-start.1
  90.9 0.0 copy-start.3
  90.9 0.0 copy-start.2
  90.9 14.3 %fusion.15 = bf16[32,3072]{1,0:T(8,128)(2,1)} fusion(f32[32,3072]{1,0:T(8,128)S(1)} %fusion.4, bf16[1,3072,4608]{2,1,0:T(8,128)(2,1)} %param.13, f32[32,4608]{1,0:T(8,128)S(1)} %fusion.10, f32[32,4608]{1,0:T(8,128)S(1)} %fusion, f32[32,4608]{1,0:T(8,128)S(1)} %fusion.6), kind=kOutput, calls=%fused_computation.18 | convolution fusion | flops 907640832 | bytes 30670848 | tf_op jit(solution)/shard_map/dot_general | solution.py:95
  105.2 0.0 reduce-scatter.5.cloned.1.call-update
  105.2 0.0 reduce-scatter.3.cloned.1.call-done
  105.2 5.0 %all-to-all-start.1 = ((bf16[4,8,1536]{2,1,0:T(8,128)(2,1)}), bf16[4,8,1536]{2,1,0:T(8,128)(2,1)S(1)}, u32[]{:S(2)}, u32[]{:S(2)}) async-start(bf16[4,8,1536]{2,1,0:T(8,128)(2,1)} %bitcast.72), calls=%async_computation.2 | async-start | bytes 196608 | tf_op jit(solution)/shard_map/all_to_all | solution.py:34
  110.3 0.1 copy.41
  110.4 0.1 reshape.87
  110.5 7.3 %reduce-scatter.5.cloned.1.call-done = bf16[32,1536]{1,0:T(8,128)(2,1)} async-done(((bf16[32,3072]{1,0:T(8,128)(2,1)}), bf16[32,1536]{1,0:T(8,128)(2,1)}) %reduce-scatter.5.cloned.1.call-update) | async-done | bytes 98320 | tf_op jit(solution)/shard_map/reduce_scatter | solution.py:30
  117.8 4.6 %all-to-all-start.3 = ((bf16[4,8,1536]{2,1,0:T(8,128)(2,1)}), bf16[4,8,1536]{2,1,0:T(8,128)(2,1)S(1)}, u32[]{:S(2)}, u32[]{:S(2)}) async-start(bf16[4,8,1536]{2,1,0:T(8,128)(2,1)} %bitcast.71), calls=%async_computation.5 | async-start | bytes 196608 | tf_op jit(solution)/shard_map/all_to_all | solution.py:34
  122.4 0.6 gather_fusion
  123.1 5.3 %all_gather.6 = bf16[16,2,3072]{2,0,1:T(8,128)(2,1)S(1)} all-gather(bf16[16,2,1536]{2,0,1:T(8,128)(2,1)S(1)} %copy.42), channel_id=1, replica_groups=mesh['dp'=4,'expert'=4,'tensor'=2] {'tensor'}, dimensions={2}, use_global_device_ids=true | all-gather | bytes 294912 | tf_op jit(solution)/shard_map/all_gather | solution.py:45
  128.4 0.1 fusion.27
  128.5 0.6 gather_fusion.1
  129.2 5.3 %all_gather.7 = bf16[16,2,3072]{2,1,0:T(2,128)(2,1)S(1)} all-gather(bf16[16,2,1536]{2,1,0:T(2,128)(2,1)S(1)} %reshape.112), channel_id=1, replica_groups=mesh['dp'=4,'expert'=4,'tensor'=2] {'tensor'}, dimensions={2}, use_global_device_ids=true | all-gather | bytes 294912 | tf_op jit(solution)/shard_map/all_gather | solution.py:45
  134.5 0.5 convert_reduce_fusion
  135.0 0.3 fusion.47
  135.4 0.5 fusion.38
  135.8 60.6 %all-reduce = (f32[3072,4]{0,1:T(4,128)}, f32[3072]{0:T(1024)}) all-reduce(f32[3072,4]{0,1:T(4,128)S(1)} %fusion.47, f32[3072]{0:T(1024)S(1)} %get-tuple-element.4), channel_id=1, replica_groups=mesh['dp'=4,'expert'=4,'tensor'=2] {'dp','expert'}, use_global_device_ids=true, to_apply=%region_7.8 | all-reduce | flops 15360 | bytes 122880 | tf_op jit(solution)/shard_map/psum | solution.py:113
  196.5 0.8 fusion.35
  (18 shorter events, 0.2 us)
Async XLA Ops:
  7.2 11.0 %copy-start = (bf16[3072,4]{0,1:T(4,128)(2,1)S(1)}, bf16[3072,4]{0,1:T(4,128)(2,1)}, u32[]{:S(2)}) copy-start(bf16[3072,4]{0,1:T(4,128)(2,1)} %param.12) | copy-start | bytes 73732
  10.9 13.9 %all-to-all-start = ((bf16[4,8,3072]{2,1,0:T(8,128)(2,1)}), bf16[4,8,3072]{2,1,0:T(8,128)(2,1)S(1)}, u32[]{:S(2)}, u32[]{:S(2)}) async-start(bf16[4,8,3072]{2,1,0:T(8,128)(2,1)} %fusion.24), calls=%async_computation | async-start | bytes 393216 | tf_op jit(solution)/shard_map/all_to_all | solution.py:23
  24.8 39.0 %all-to-all-start.2 = ((bf16[4,8,3072]{2,1,0:T(8,128)(2,1)}), bf16[4,8,3072]{2,1,0:T(8,128)(2,1)S(1)}, u32[]{:S(2)}, u32[]{:S(2)}) async-start(bf16[4,8,3072]{2,1,0:T(8,128)(2,1)} %fusion.23), calls=%async_computation.3 | async-start | bytes 393216 | tf_op jit(solution)/shard_map/all_to_all | solution.py:23
  28.1 77.1 %reduce-scatter.3.cloned.1.call-start = ((), (), s32[]{:S(2)}) async-start(), calls=%async_computation.6 | async-start | bytes 294912 | tf_op jit(solution)/shard_map/reduce_scatter | solution.py:30
  63.6 54.2 %reduce-scatter.5.cloned.1.call-start = ((), (), s32[]{:S(2)}) async-start(), calls=%async_computation.7 | async-start | bytes 294912 | tf_op jit(solution)/shard_map/reduce_scatter | solution.py:30
  90.9 19.4 %copy-start.4 = (s32[16,2]{0,1:T(2,128)S(1)}, s32[16,2]{0,1:T(2,128)}, u32[]{:S(2)}) copy-start(s32[16,2]{0,1:T(2,128)} %param.16) | copy-start | bytes 388
  90.9 44.5 %copy-start.1 = (bf16[16,3072]{1,0:T(8,128)(2,1)S(1)}, bf16[16,3072]{1,0:T(8,128)(2,1)}, u32[]{:S(2)}) copy-start(bf16[16,3072]{1,0:T(8,128)(2,1)} %param.9) | copy-start | bytes 294916
  90.9 44.5 %copy-start.3 = (f32[3072]{0:T(1024)S(1)}, f32[3072]{0:T(1024)}, u32[]{:S(2)}) copy-start(f32[3072]{0:T(1024)} %param.11) | copy-start | bytes 36868
  90.9 105.5 %copy-start.2 = (bf16[16,3072]{1,0:T(8,128)(2,1)S(1)}, bf16[16,3072]{1,0:T(8,128)(2,1)}, u32[]{:S(2)}) copy-start(bf16[16,3072]{1,0:T(8,128)(2,1)} %param.10) | copy-start | bytes 294916
  105.2 12.5 %all-to-all-start.1 = ((bf16[4,8,1536]{2,1,0:T(8,128)(2,1)}), bf16[4,8,1536]{2,1,0:T(8,128)(2,1)S(1)}, u32[]{:S(2)}, u32[]{:S(2)}) async-start(bf16[4,8,1536]{2,1,0:T(8,128)(2,1)} %bitcast.72), calls=%async_computation.2 | async-start | bytes 196608 | tf_op jit(solution)/shard_map/all_to_all | solution.py:34
  117.8 10.8 %all-to-all-start.3 = ((bf16[4,8,1536]{2,1,0:T(8,128)(2,1)}), bf16[4,8,1536]{2,1,0:T(8,128)(2,1)S(1)}, u32[]{:S(2)}, u32[]{:S(2)}) async-start(bf16[4,8,1536]{2,1,0:T(8,128)(2,1)} %bitcast.71), calls=%async_computation.5 | async-start | bytes 196608 | tf_op jit(solution)/shard_map/all_to_all | solution.py:34
Sparse Core Ops, SparseCore 0:
  63.7 12.3 reduce-scatter.2
  105.3 12.3 reduce-scatter.4
where the time goes:
time: 205 us; the launch traced here: 204 us
  matrix products  79.6 us (39%)
  blocking collectives  71.2 us (35%)
  starting transfers between devices  19.6 us (10%)
  between operations  14.2 us (7%)
  waiting for transfers between devices  10.3 us (5%)
  other arithmetic  6.49 us (3%)
  local copies, waits for them, and re-layouts  2.68 us (1%)
    psum x1, blocking collectives, shards(): lax.psum((router_part, gain_part), ('dp', 'expert'))  60.6 us
    dot_general x1, matrix products, shards(): jnp.dot(grad_gate, gate_matrix.T, preferred_element_type=jnp.float32)  14.3 us
    dot_general x1, matrix products, shards(): jnp.dot(grad_outputs, down_matrix.T, preferred_element_type=jnp.float32)  13.6 us
    dot_general x1, matrix products, shards(): jnp.dot(grad_up, up_matrix.T, preferred_element_type=jnp.float32)  13.5 us
    dot_general x1, matrix products, shards(): jnp.dot(activated, down_matrix, preferred_element_type=jnp.float32)  12.3 us
    dot_general x1, matrix products, shards(): gate_pre = jnp.dot(inputs, gate_matrix, preferred_element_type=jnp.float32)  11.5 us
    dot_general x1, matrix products, shards(): up_pre = jnp.dot(inputs, up_matrix, preferred_element_type=jnp.float32)  11.5 us
    all_gather x2, blocking collectives, from_experts(): lax.all_gather(picked.astype(jnp.bfloat16), 'tensor', axis=2, tiled=True)  10.6 us
  transfers between devices with their start and end apart: 6, of which 2 were waited for; matrix products, arithmetic and copies ran while one was open for 40% of the time, Pallas kernels for 0%

commit v1 on v0

--- a/solution.py
+++ b/solution.py
@@ -1,9 +1,19 @@
+import functools
 import jax
 import jax.numpy as jnp
 from jax import lax
 from jax.sharding import PartitionSpec as P
 
 epsilon = 1e-05
+
+
+def take_run(arr, axis_id, axis_name):
+    for dev_j in (axis_id, axis_name):
+        arr = jax.lax.psum(arr, dev_j)
+    return arr
+
+
+roads_move = functools.partial(take_run, axis_id="expert", axis_name="dp")
 
 
 def pack_rows(select, values):
@@ -110,7 +120,7 @@
         normed.astype(jnp.float32).T, grad_logits, precision=lax.Precision.HIGHEST
     )
     gain_part = jnp.sum(grad_normed * floats * inv_rms, axis=0)
-    grad_router, grad_gain = lax.psum((router_part, gain_part), ("dp", "expert"))
+    grad_router, grad_gain = roads_move((router_part, gain_part))
     grad_scaled = grad_normed * gain
     cubed = inv_rms * inv_rms * inv_rms
     grad_tokens = (

time: 205 us -> 176 us (0.86)
  blocking collectives: 71.2 us -> 42 us
    psum x1 -> x2, blocking collectives: 60.6 us -> 31.4 us  [take_run(): arr = jax.lax.psum(arr, dev_j)]
  transfers between devices with their start and end apart: 6 -> 6, of which waited for: 2 -> 2; matrix products, arithmetic and copies ran while one was open for 40% -> 47% of each run, Pallas kernels for 0% -> 0%
where the time goes in v1:
time: 176 us; the launch traced here: 175 us
  matrix products  79.6 us (45%)
  blocking collectives  42 us (24%)
  starting transfers between devices  19.6 us (11%)
  between operations  14.2 us (8%)
  waiting for transfers between devices  10.3 us (6%)
  other arithmetic  6.49 us (4%)
  local copies, waits for them, and re-layouts  2.68 us (2%)
    psum x2, blocking collectives, take_run(): arr = jax.lax.psum(arr, dev_j)  31.4 us
    dot_general x1, matrix products, shards(): jnp.dot(grad_gate, gate_matrix.T, preferred_element_type=jnp.float32)  14.3 us
    dot_general x1, matrix products, shards(): jnp.dot(grad_outputs, down_matrix.T, preferred_element_type=jnp.float32)  13.6 us
    dot_general x1, matrix products, shards(): jnp.dot(grad_up, up_matrix.T, preferred_element_type=jnp.float32)  13.5 us
    dot_general x1, matrix products, shards(): jnp.dot(activated, down_matrix, preferred_element_type=jnp.float32)  12.3 us
    dot_general x1, matrix products, shards(): gate_pre = jnp.dot(inputs, gate_matrix, preferred_element_type=jnp.float32)  11.5 us
    dot_general x1, matrix products, shards(): up_pre = jnp.dot(inputs, up_matrix, preferred_element_type=jnp.float32)  11.5 us
    all_gather x2, blocking collectives, from_experts(): lax.all_gather(picked.astype(jnp.bfloat16), 'tensor', axis=2, tiled=True)  10.6 us
  transfers between devices with their start and end apart: 6, of which 2 were waited for; matrix products, arithmetic and copies ran while one was open for 47% of the time, Pallas kernels for 0%

profile of v1, /device:TPU:0, one launch (start us, length us, event | category | flops | bytes accessed | tf_op | source)
XLA Modules:
  0.0 174.9 jit_solution(1627335754137936958)
XLA Ops:
  7.2 0.0 copy-start
  7.2 1.0 fusion.29
  8.2 0.7 compare_select_fusion
  8.9 1.0 fusion.31
  9.9 1.0 fusion.24
  10.9 6.3 %all-to-all-start = ((bf16[4,8,3072]{2,1,0:T(8,128)(2,1)}), bf16[4,8,3072]{2,1,0:T(8,128)(2,1)S(1)}, u32[]{:S(2)}, u32[]{:S(2)}) async-start(bf16[4,8,3072]{2,1,0:T(8,128)(2,1)} %fusion.24), calls=%async_computation | async-start | bytes 393216 | tf_op jit(solution)/shard_map/all_to_all | solution.py:33
  17.3 0.7 bitcast_or_fusion
  17.9 0.1 copy.39
  18.0 0.1 reshape.101
  18.1 0.1 fusion.59
  18.3 0.8 gather_fusion.2
  19.0 0.1 reshape.104
  19.1 0.1 copy.40
  19.2 0.7 and_select_fusion
  19.9 0.9 convert_element_type.70
  20.8 1.0 fusion.23
  21.8 2.9 %all-to-all-done = bf16[4,8,3072]{2,1,0:T(8,128)(2,1)S(1)} async-done(((bf16[4,8,3072]{2,1,0:T(8,128)(2,1)}), bf16[4,8,3072]{2,1,0:T(8,128)(2,1)S(1)}, u32[]{:S(2)}, u32[]{:S(2)}) %all-to-all-start) | async-done | bytes 196640 | tf_op jit(solution)/shard_map/all_to_all | solution.py:33
  24.8 3.4 %all-to-all-start.2 = ((bf16[4,8,3072]{2,1,0:T(8,128)(2,1)}), bf16[4,8,3072]{2,1,0:T(8,128)(2,1)S(1)}, u32[]{:S(2)}, u32[]{:S(2)}) async-start(bf16[4,8,3072]{2,1,0:T(8,128)(2,1)} %fusion.23), calls=%async_computation.3 | async-start | bytes 393216 | tf_op jit(solution)/shard_map/all_to_all | solution.py:33
  28.1 0.0 reduce-scatter.3.cloned.1.call-start
  28.2 11.5 %fusion.10 = f32[32,4608]{1,0:T(8,128)S(1)} fusion(bf16[1,3072,4608]{2,1,0:T(8,128)(2,1)} %param.13, bf16[4,8,3072]{2,1,0:T(8,128)(2,1)S(1)} %all-to-all-done), kind=kOutput, calls=%fused_computation.13 | convolution fusion | flops 905969664 | bytes 29097984 | tf_op jit(solution)/shard_map/dot_general | solution.py:86
  39.7 11.5 %fusion.6 = f32[32,4608]{1,0:T(8,128)S(1)} fusion(bf16[1,3072,4608]{2,1,0:T(8,128)(2,1)} %param.14, bf16[4,8,3072]{2,1,0:T(8,128)(2,1)S(1)} %all-to-all-done), kind=kOutput, calls=%fused_computation.9 | convolution fusion | flops 905969664 | bytes 29097984 | tf_op jit(solution)/shard_map/dot_general | solution.py:87
  51.2 12.3 %fusion.20 = bf16[32,3072]{1,0:T(8,128)(2,1)} fusion(bf16[1,4608,3072]{2,1,0:T(8,128)(2,1)} %param.15, f32[32,4608]{1,0:T(8,128)S(1)} %fusion.6, f32[32,4608]{1,0:T(8,128)S(1)} %fusion.10), kind=kOutput, calls=%fused_computation.21 | convolution fusion | flops 906952704 | bytes 29687808 | tf_op jit(solution)/shard_map/dot_general | solution.py:90
  63.6 0.0 reduce-scatter.3.cloned.1.call-update
  63.6 0.2 reduce-scatter.5.cloned.1.call-start
  63.8 13.6 %fusion = f32[32,4608]{1,0:T(8,128)S(1)} fusion(bf16[1,4608,3072]{2,1,0:T(8,128)(2,1)} %param.15, bf16[4,8,3072]{2,1,0:T(8,128)(2,1)S(1)} %all-to-all-done.2), kind=kOutput, calls=%fused_computation.3 | convolution fusion | flops 905969664 | bytes 29097984 | tf_op jit(solution)/shard_map/dot_general | solution.py:99
  77.4 13.5 %fusion.4 = f32[32,3072]{1,0:T(8,128)S(1)} fusion(bf16[1,3072,4608]{2,1,0:T(8,128)(2,1)} %param.14, f32[32,4608]{1,0:T(8,128)S(1)} %fusion, f32[32,4608]{1,0:T(8,128)S(1)} %fusion.10), kind=kOutput, calls=%fused_computation.7 | convolution fusion | flops 906854400 | bytes 29884416 | tf_op jit(solution)/shard_map/dot_general | solution.py:105
  90.9 0.0 copy-start.1
  90.9 0.0 copy-start.3
  90.9 0.0 copy-start.2
  90.9 14.3 %fusion.15 = bf16[32,3072]{1,0:T(8,128)(2,1)} fusion(f32[32,3072]{1,0:T(8,128)S(1)} %fusion.4, bf16[1,3072,4608]{2,1,0:T(8,128)(2,1)} %param.13, f32[32,4608]{1,0:T(8,128)S(1)} %fusion.10, f32[32,4608]{1,0:T(8,128)S(1)} %fusion, f32[32,4608]{1,0:T(8,128)S(1)} %fusion.6), kind=kOutput, calls=%fused_computation.18 | convolution fusion | flops 907640832 | bytes 30670848 | tf_op jit(solution)/shard_map/dot_general | solution.py:105
  105.2 0.0 reduce-scatter.5.cloned.1.call-update
  105.2 0.0 reduce-scatter.3.cloned.1.call-done
  105.2 5.0 %all-to-all-start.1 = ((bf16[4,8,1536]{2,1,0:T(8,128)(2,1)}), bf16[4,8,1536]{2,1,0:T(8,128)(2,1)S(1)}, u32[]{:S(2)}, u32[]{:S(2)}) async-start(bf16[4,8,1536]{2,1,0:T(8,128)(2,1)} %bitcast.72), calls=%async_computation.2 | async-start | bytes 196608 | tf_op jit(solution)/shard_map/all_to_all | solution.py:44
  110.3 0.1 copy.41
  110.3 0.1 reshape.87
  110.4 7.3 %reduce-scatter.5.cloned.1.call-done = bf16[32,1536]{1,0:T(8,128)(2,1)} async-done(((bf16[32,3072]{1,0:T(8,128)(2,1)}), bf16[32,1536]{1,0:T(8,128)(2,1)}) %reduce-scatter.5.cloned.1.call-update) | async-done | bytes 98320 | tf_op jit(solution)/shard_map/reduce_scatter | solution.py:40
  117.8 4.6 %all-to-all-start.3 = ((bf16[4,8,1536]{2,1,0:T(8,128)(2,1)}), bf16[4,8,1536]{2,1,0:T(8,128)(2,1)S(1)}, u32[]{:S(2)}, u32[]{:S(2)}) async-start(bf16[4,8,1536]{2,1,0:T(8,128)(2,1)} %bitcast.71), calls=%async_computation.5 | async-start | bytes 196608 | tf_op jit(solution)/shard_map/all_to_all | solution.py:44
  122.4 0.6 gather_fusion
  123.1 5.3 %all_gather.6 = bf16[16,2,3072]{2,0,1:T(8,128)(2,1)S(1)} all-gather(bf16[16,2,1536]{2,0,1:T(8,128)(2,1)S(1)} %copy.42), channel_id=1, replica_groups=mesh['dp'=4,'expert'=4,'tensor'=2] {'tensor'}, dimensions={2}, use_global_device_ids=true | all-gather | bytes 294912 | tf_op jit(solution)/shard_map/all_gather | solution.py:55
  128.4 0.1 fusion.27
  128.5 0.6 gather_fusion.1
  129.2 5.3 %all_gather.7 = bf16[16,2,3072]{2,1,0:T(2,128)(2,1)S(1)} all-gather(bf16[16,2,1536]{2,1,0:T(2,128)(2,1)S(1)} %reshape.112), channel_id=1, replica_groups=mesh['dp'=4,'expert'=4,'tensor'=2] {'tensor'}, dimensions={2}, use_global_device_ids=true | all-gather | bytes 294912 | tf_op jit(solution)/shard_map/all_gather | solution.py:55
  134.5 0.5 convert_reduce_fusion
  135.0 0.3 fusion.47
  135.4 0.5 fusion.38
  135.8 20.1 %all-reduce = (f32[3072,4]{0,1:T(4,128)S(1)}, f32[3072]{0:T(1024)S(1)}) all-reduce(f32[3072,4]{0,1:T(4,128)S(1)} %fusion.47, f32[3072]{0:T(1024)S(1)} %get-tuple-element.4), channel_id=1, replica_groups=mesh['dp'=4,'expert'=4,'tensor'=2] {'expert'}, use_global_device_ids=true, to_apply=%region_7.8 | all-reduce | flops 15360 | bytes 122880 | tf_op jit(solution)/shard_map/psum | solution.py:12
  156.0 11.3 %all-reduce.1 = (f32[3072,4]{0,1:T(4,128)}, f32[3072]{0:T(1024)}) all-reduce(f32[3072,4]{0,1:T(4,128)S(1)} %get-tuple-element.8, f32[3072]{0:T(1024)S(1)} %get-tuple-element.9), channel_id=1, replica_groups=mesh['dp'=4,'expert'=4,'tensor'=2] {'dp'}, use_global_device_ids=true, to_apply=%region_8.9 | all-reduce | flops 15360 | bytes 122880 | tf_op jit(solution)/shard_map/psum | solution.py:12
  167.2 0.8 fusion.35
  (19 shorter events, 0.2 us)
Async XLA Ops:
  7.2 11.0 %copy-start = (bf16[3072,4]{0,1:T(4,128)(2,1)S(1)}, bf16[3072,4]{0,1:T(4,128)(2,1)}, u32[]{:S(2)}) copy-start(bf16[3072,4]{0,1:T(4,128)(2,1)} %param.12) | copy-start | bytes 73732
  10.9 13.9 %all-to-all-start = ((bf16[4,8,3072]{2,1,0:T(8,128)(2,1)}), bf16[4,8,3072]{2,1,0:T(8,128)(2,1)S(1)}, u32[]{:S(2)}, u32[]{:S(2)}) async-start(bf16[4,8,3072]{2,1,0:T(8,128)(2,1)} %fusion.24), calls=%async_computation | async-start | bytes 393216 | tf_op jit(solution)/shard_map/all_to_all | solution.py:33
  24.8 39.0 %all-to-all-start.2 = ((bf16[4,8,3072]{2,1,0:T(8,128)(2,1)}), bf16[4,8,3072]{2,1,0:T(8,128)(2,1)S(1)}, u32[]{:S(2)}, u32[]{:S(2)}) async-start(bf16[4,8,3072]{2,1,0:T(8,128)(2,1)} %fusion.23), calls=%async_computation.3 | async-start | bytes 393216 | tf_op jit(solution)/shard_map/all_to_all | solution.py:33
  28.1 77.1 %reduce-scatter.3.cloned.1.call-start = ((), (), s32[]{:S(2)}) async-start(), calls=%async_computation.6 | async-start | bytes 294912 | tf_op jit(solution)/shard_map/reduce_scatter | solution.py:40
  63.6 54.2 %reduce-scatter.5.cloned.1.call-start = ((), (), s32[]{:S(2)}) async-start(), calls=%async_computation.7 | async-start | bytes 294912 | tf_op jit(solution)/shard_map/reduce_scatter | solution.py:40
  90.9 19.4 %copy-start.4 = (s32[16,2]{0,1:T(2,128)S(1)}, s32[16,2]{0,1:T(2,128)}, u32[]{:S(2)}) copy-start(s32[16,2]{0,1:T(2,128)} %param.16) | copy-start | bytes 388
  90.9 44.5 %copy-start.1 = (bf16[16,3072]{1,0:T(8,128)(2,1)S(1)}, bf16[16,3072]{1,0:T(8,128)(2,1)}, u32[]{:S(2)}) copy-start(bf16[16,3072]{1,0:T(8,128)(2,1)} %param.9) | copy-start | bytes 294916
  90.9 44.4 %copy-start.3 = (f32[3072]{0:T(1024)S(1)}, f32[3072]{0:T(1024)}, u32[]{:S(2)}) copy-start(f32[3072]{0:T(1024)} %param.11) | copy-start | bytes 36868
  90.9 76.3 %copy-start.2 = (bf16[16,3072]{1,0:T(8,128)(2,1)S(1)}, bf16[16,3072]{1,0:T(8,128)(2,1)}, u32[]{:S(2)}) copy-start(bf16[16,3072]{1,0:T(8,128)(2,1)} %param.10) | copy-start | bytes 294916
  105.2 12.5 %all-to-all-start.1 = ((bf16[4,8,1536]{2,1,0:T(8,128)(2,1)}), bf16[4,8,1536]{2,1,0:T(8,128)(2,1)S(1)}, u32[]{:S(2)}, u32[]{:S(2)}) async-start(bf16[4,8,1536]{2,1,0:T(8,128)(2,1)} %bitcast.72), calls=%async_computation.2 | async-start | bytes 196608 | tf_op jit(solution)/shard_map/all_to_all | solution.py:44
  117.8 10.8 %all-to-all-start.3 = ((bf16[4,8,1536]{2,1,0:T(8,128)(2,1)}), bf16[4,8,1536]{2,1,0:T(8,128)(2,1)S(1)}, u32[]{:S(2)}, u32[]{:S(2)}) async-start(bf16[4,8,1536]{2,1,0:T(8,128)(2,1)} %bitcast.71), calls=%async_computation.5 | async-start | bytes 196608 | tf_op jit(solution)/shard_map/all_to_all | solution.py:44
Sparse Core Ops, SparseCore 0:
  63.7 12.3 reduce-scatter.2
  105.3 12.3 reduce-scatter.4
